TPU v7x, 256 devices: a whole 4x4x8 slice. The times are simulated.
256 devices in a mesh: row: 32 (over z, x), col: 8 (over y, core).
Axes of the slice: x: 4, y: 4, z: 8, core: 2. Of those that a mesh axis runs over, the one named last changes fastest.
Arguments:
- integrals: bfloat16 [65536, 8192], P('row', 'col'), may hold values from -0.0234375 to 0.0234375
- lambda2: bfloat16 [2016, 65536], P('col', 'row'), may hold values from -6 to 6
- source_terms: float32 [2016, 8192], P('row', 'col'), may hold values from -6 to 6
- hist_amp: bfloat16 [5, 2016, 8192], P(None, 'row', 'col'), may hold values from -6 to 6
- hist_err: bfloat16 [5, 2016, 8192], P(None, 'row', 'col'), may hold values from -64 to 64
- eps_occ: float32 [64], replicated, may hold values from -1 to -0.3
- eps_vir: float32 [800], replicated, may hold values from 0.1 to 1
- occ_pair: int32 [2, 2016], P(None, 'row'), may hold values from 0 to 63, as said below
- vir_pair: int32 [2, 8192], P(None, 'col'), may hold values from 0 to 799, as said below
Outputs:
- updated: float32 [2016, 8192], P('row', 'col')
Inputs may be any that keep to these rules, and one draw needn't show every extreme that they name: `occ_pair`: every pair i < j of the 64 occupied orbitals appears exactly once, in some order. `vir_pair`: in every column the first orbital is smaller than the second.
All inputs are finite; a program needn't handle non-finite values.
Results may differ from a plain program's by a relative error of at most 0.0003.
Values may be sent and summed in bfloat16 or wider, within the bound.
A program may use at most 64 MiB of HBM per device.

v0:
```python
import jax
import jax.numpy as jnp
from jax import lax
from jax.sharding import PartitionSpec as P

precise = lax.Precision.HIGHEST


def pair_energy(pairs, energies):
    levels = jnp.arange(energies.shape[0], dtype=jnp.int32)
    first = jnp.sum(jnp.where(pairs[0][:, None] == levels[None, :], energies[None, :], 0.0), axis=1)
    second = jnp.sum(
        jnp.where(pairs[1][:, None] == levels[None, :], energies[None, :], 0.0), axis=1
    )
    return first + second


def diis_weights(correlation):
    factor = jnp.linalg.cholesky(correlation)
    order = correlation.shape[0]
    forward = []
    for k in range(order):
        running = jnp.ones((), correlation.dtype)
        for m in range(k):
            running = running - factor[k, m] * forward[m]
        forward.append(running / factor[k, k])
    backward = [None] * order
    for k in reversed(range(order)):
        running = forward[k]
        for m in range(k + 1, order):
            running = running - factor[m, k] * backward[m]
        backward[k] = running / factor[k, k]
    solved = jnp.stack(backward)
    return solved / jnp.sum(solved)


def on_device(
    integrals, lambda2, source_terms, hist_amp, hist_err, eps_occ, eps_vir, occ_pair, vir_pair
):
    stored_count = hist_err.shape[0]
    flat_stored = hist_err.astype(jnp.float32).reshape(stored_count, -1)
    all_cols = lax.all_gather(lambda2, "col", axis=0, tiled=True)
    ladder = lax.psum_scatter(
        jnp.dot(all_cols, integrals, preferred_element_type=jnp.float32),
        "row",
        scatter_dimension=0,
        tiled=True,
    )
    denominator = pair_energy(occ_pair, eps_occ)[:, None] - pair_energy(vir_pair, eps_vir)[None, :]
    raw_update = (source_terms + ladder) / denominator
    err_new = raw_update - hist_amp[0].astype(jnp.float32)
    flat_new = err_new.reshape(1, -1)
    stacked = jnp.concatenate([flat_stored, flat_new], axis=0)
    correlation = lax.psum(jnp.dot(stacked, stacked.T, precision=precise), ("row", "col"))
    weights = diis_weights(correlation)
    updated = weights[stored_count] * raw_update
    for k in range(stored_count):
        updated = updated + weights[k] * hist_amp[k].astype(jnp.float32)
    return updated


def solution(mesh):
    placed = (
        P("row", "col"),
        P("col", "row"),
        P("row", "col"),
        P(None, "row", "col"),
        P(None, "row", "col"),
        P(),
        P(),
        P(None, "row"),
        P(None, "col"),
    )
    return jax.shard_map(
        on_device, mesh=mesh, in_specs=placed, out_specs=P("row", "col"), check_vma=False
    )
```

profile of v0, /device:TPU:1, one launch (start us, length us, event | category | flops | bytes accessed | tf_op | source)
XLA Modules:
  0.0 320.9 jit_solution(15406420744793112163)
XLA Ops:
  6.5 0.0 all-gather.3.cloned.1.call-start
  6.5 0.7 all-gather.3.cloned.1.call-update
  7.3 0.8 fusion.14
  8.0 1.5 select_reduce_fusion
  9.6 1.2 convert_bitcast_fusion
  10.8 54.8 %all-gather.3.cloned.1.call-done = bf16[8,252,2048]{2,1,0:T(8,128)(2,1)} async-done(((bf16[1,252,2048]{2,1,0:T(8,128)(2,1)}), bf16[8,252,2048]{2,1,0:T(8,128)(2,1)}) %all-gather.3.cloned.1.call-update) | async-done | bytes 8257552 | tf_op jit(solution)/shard_map/all_gather | solution.py:42
  65.7 7.5 %reshape.68 = bf16[2016,2048]{1,0:T(8,128)(2,1)} reshape(bf16[8,252,2048]{2,1,0:T(8,128)(2,1)} %all-gather.3.cloned.1.call-done) | data formatting | bytes 16515072
  73.1 14.2 %fusion.18 = f32[2016,1024]{1,0:T(8,128)} fusion(bf16[2016,2048]{1,0:T(8,128)(2,1)} %reshape.68, bf16[2048,1024]{1,0:T(8,128)(2,1)} %param.9), kind=kOutput, calls=%fused_computation.38 | convolution fusion | flops 8455716864 | bytes 20709376 | tf_op jit(solution)/shard_map/dot_general | solution.py:44
  87.4 0.0 copy-start.3
  87.4 100.2 %fusion = f32[64,1024]{1,0:T(8,128)S(1)} fusion(f32[2016,1024]{1,0:T(8,128)} %fusion.18), kind=kCustom, calls=%all-reduce-scatter | all-reduce-scatter fusion | flops 2097153 | bytes 8520704
  187.6 0.0 copy-start
  187.6 0.0 copy-start.5
  187.6 0.0 copy-start.4
  187.6 2.3 collective-permute-start
  189.9 0.0 copy-done.3
  190.0 0.0 copy-done
  190.0 0.8 copy.19
  190.8 0.0 copy-done.5
  190.8 0.0 copy-start.1
  190.8 0.0 copy-start.2
  190.8 0.6 dynamic-slice.4
  191.9 0.0 copy-done.4
  192.0 0.2 select_reduce_fusion.2
  192.2 0.0 collective-permute-done
  192.2 2.0 concatenate.4
  194.2 1.1 fusion.5
  195.3 0.3 copy.20
  195.6 4.5 %fusion.1 = f32[6,6]{0,1:T(8,128)S(1)} fusion(f32[1,64512]{1,0:T(1,128)S(1)} %bitcast.70, f32[5,64512]{1,0:T(8,128)S(1)} %bitcast.68), kind=kOutput, calls=%fused_computation.4 | convolution fusion | flops 28256256 | bytes 1548432 | tf_op jit(solution)/shard_map/dot_general | solution.py:54
  200.1 78.7 %psum.7 = f32[6,6]{0,1:T(8,128)S(1)} all-reduce(f32[6,6]{0,1:T(8,128)S(1)} %fusion.1), channel_id=1, replica_groups=mesh['row'=32,'col'=8] {'row','col'}, use_global_device_ids=true, to_apply=%region_5.6 | all-reduce | flops 36 | bytes 288 | tf_op jit(solution)/shard_map/psum | solution.py:54
  278.8 0.1 copy.17
  278.9 0.5 cholesky.18
  279.4 0.6 compare_reduce_fusion
  280.1 0.6 select_select_fusion
  280.7 0.6 fusion.16
  281.3 0.7 fusion.15
  308.7 0.1 stack.27
  308.7 0.7 fusion.17
  309.4 0.0 copy-done.1
  309.4 0.0 copy-done.2
  309.4 4.6 %fusion.10 = f32[63,1024]{1,0:T(8,128)} fusion(bf16[5,63,1024]{2,1,0:T(8,128)(2,1)S(1)} %copy-done.2, f32[]{:T(128)} %bitcast.43, f32[]{:T(128)} %bitcast.41, f32[]{:T(128)} %bitcast.39, f32[]{:T(128)} %bitcast.37, f32[]{:T(128)} %bitcast.35, f32[]{:T(128)} %bitcast.34, f32[1024]{0:T(1024)S(1)} %add.47, f32[63]{0:T(128)S(1)} %add.46, ...), kind=kLoop, calls=%fused_computation.16 | loop fusion | flops 1225728 | bytes 1423640 | tf_op jit(solution)/shard_map/add | solution.py:58
  (7 shorter events, 0.1 us)
Async XLA Ops:
  6.5 59.1 %all-gather.3.cloned.1.call-start = ((), (), s32[]{:S(2)}) async-start(), calls=%async_computation | async-start | bytes 9437184 | tf_op jit(solution)/shard_map/all_gather | solution.py:42
  87.4 102.6 %copy-start.3 = (s32[2,63]{1,0:T(2,128)S(1)}, s32[2,63]{1,0:T(2,128)}, u32[]{:S(2)}) copy-start(s32[2,63]{1,0:T(2,128)} %param.16) | copy-start | bytes 1516
  187.6 2.4 copy-start
  187.6 3.2 copy-start.5
  187.6 4.3 %copy-start.4 = (f32[64]{0:T(128)S(1)}, f32[64]{0:T(128)}, u32[]{:S(2)}) copy-start(f32[64]{0:T(128)} %param.14) | copy-start | bytes 772
  187.6 4.5 %collective-permute-start = (f32[31,1024]{1,0:T(8,128)S(1)}, f32[31,1024]{1,0:T(8,128)}, u32[]{:S(2)}, u32[]{:S(2)}) collective-permute-start(f32[31,1024]{1,0:T(8,128)S(1)} %slice.172), channel_id=1, source_target_pairs={{0,8},{8,16},{16,24},{24,32},{32,40},{40,48},{48,56},{56,64},{64,7... | collective-permute-start | bytes 380936
  190.8 118.6 %copy-start.1 = (f32[63,1024]{1,0:T(8,128)S(1)}, f32[63,1024]{1,0:T(8,128)}, u32[]{:S(2)}) copy-start(f32[63,1024]{1,0:T(8,128)} %param.11) | copy-start | bytes 774148
  190.8 118.6 %copy-start.2 = (bf16[5,63,1024]{2,1,0:T(8,128)(2,1)S(1)}, bf16[5,63,1024]{2,1,0:T(8,128)(2,1)}, u32[]{:S(2)}) copy-start(bf16[5,63,1024]{2,1,0:T(8,128)(2,1)} %param.12) | copy-start | bytes 1935364
Sparse Core Ops, SparseCore 0:
  9.2 56.4 all-gather.2
where the time goes:
time: 322 us; the launch traced here: 321 us
  blocking collectives  179 us (56%)
  waiting for transfers between devices  55.6 us (17%)
  between operations  40.7 us (13%)
  matrix products  18.7 us (6%)
  local copies, waits for them, and re-layouts  14.1 us (4%)
  other arithmetic  10.6 us (3%)
    unnamed x1, blocking collectives  100 us
    psum x1, blocking collectives, on_device(): lax.psum(jnp.dot(stacked, stacked.T, precision=precise), ('row', 'col'))  78.7 us
    all_gather x1, waiting for transfers between devices, on_device(): all_cols = lax.all_gather(lambda2, 'col', axis=0, tiled=True)  54.8 us
    dot_general x1, matrix products, on_device(): jnp.dot(all_cols, integrals, preferred_element_type=jnp.float32)  14.2 us
    unnamed x18, local copies, waits for them, and re-layouts  11.2 us
  transfers between devices with their start and end apart: 2, of which 1 were waited for; matrix products, arithmetic and copies ran while one was open for 2% of the time, Pallas kernels for 0%

commit v1 on v0

--- a/solution.py
+++ b/solution.py
@@ -51,7 +51,8 @@
     err_new = raw_update - hist_amp[0].astype(jnp.float32)
     flat_new = err_new.reshape(1, -1)
     stacked = jnp.concatenate([flat_stored, flat_new], axis=0)
-    correlation = lax.psum(jnp.dot(stacked, stacked.T, precision=precise), ("row", "col"))
+    array_in = jnp.dot(stacked, stacked.T, precision=precise)
+    correlation = jax.lax.psum(jax.lax.psum(array_in, "col"), "row")
     weights = diis_weights(correlation)
     updated = weights[stored_count] * raw_update
     for k in range(stored_count):

time: 322 us -> 330 us (1.025)
  the two profiles are of different devices: /device:TPU:1 before, /device:TPU:130 now
where the time goes in v1:
time: 330 us; the launch traced here: 329 us
  blocking collectives  186 us (56%)
  waiting for transfers between devices  56 us (17%)
  between operations  40.7 us (12%)
  matrix products  18.7 us (6%)
  local copies, waits for them, and re-layouts  14.1 us (4%)
  other arithmetic  10.6 us (3%)
    unnamed x1, blocking collectives  99.1 us
    psum x2, blocking collectives, on_device(): correlation = jax.lax.psum(jax.lax.psum(array_in, 'col'), 'row')  87.4 us
    all_gather x1, waiting for transfers between devices, on_device(): all_cols = lax.all_gather(lambda2, 'col', axis=0, tiled=True)  52.1 us
    dot_general x1, matrix products, on_device(): jnp.dot(all_cols, integrals, preferred_element_type=jnp.float32)  14.2 us
    unnamed x18, local copies, waits for them, and re-layouts  11.1 us
  transfers between devices with their start and end apart: 2, of which 2 were waited for; matrix products, arithmetic and copies ran while one was open for 2% of the time, Pallas kernels for 0%

profile of v1, /device:TPU:130, one launch (start us, length us, event | category | flops | bytes accessed | tf_op | source)
XLA Modules:
  0.0 328.7 jit_solution(9233556880754398183)
XLA Ops:
  6.5 0.0 all-gather.3.cloned.1.call-start
  6.5 0.7 all-gather.3.cloned.1.call-update
  7.3 0.8 fusion.14
  8.0 1.5 select_reduce_fusion
  9.6 1.2 convert_bitcast_fusion
  10.8 52.1 %all-gather.3.cloned.1.call-done = bf16[8,252,2048]{2,1,0:T(8,128)(2,1)} async-done(((bf16[1,252,2048]{2,1,0:T(8,128)(2,1)}), bf16[8,252,2048]{2,1,0:T(8,128)(2,1)}) %all-gather.3.cloned.1.call-update) | async-done | bytes 8257552 | tf_op jit(solution)/shard_map/all_gather | solution.py:42
  62.9 7.5 %reshape.68 = bf16[2016,2048]{1,0:T(8,128)(2,1)} reshape(bf16[8,252,2048]{2,1,0:T(8,128)(2,1)} %all-gather.3.cloned.1.call-done) | data formatting | bytes 16515072
  70.4 14.2 %fusion.18 = f32[2016,1024]{1,0:T(8,128)} fusion(bf16[2016,2048]{1,0:T(8,128)(2,1)} %reshape.68, bf16[2048,1024]{1,0:T(8,128)(2,1)} %param.9), kind=kOutput, calls=%fused_computation.38 | convolution fusion | flops 8455716864 | bytes 20709376 | tf_op jit(solution)/shard_map/dot_general | solution.py:44
  84.6 0.0 copy-start.3
  84.6 99.1 %fusion = f32[64,1024]{1,0:T(8,128)S(1)} fusion(f32[2016,1024]{1,0:T(8,128)} %fusion.18), kind=kCustom, calls=%all-reduce-scatter | all-reduce-scatter fusion | flops 2097153 | bytes 8520704
  183.7 0.0 copy-start
  183.8 0.0 copy-start.5
  183.8 0.0 copy-start.4
  183.8 2.1 collective-permute-start
  185.9 0.0 copy-done.3
  185.9 0.0 copy-done
  185.9 0.8 copy.19
  186.7 0.0 copy-done.5
  186.7 0.0 copy-start.1
  186.7 0.0 copy-start.2
  186.7 0.6 dynamic-slice.4
  187.9 0.0 copy-done.4
  187.9 0.2 select_reduce_fusion.2
  188.1 3.1 collective-permute-done
  191.2 2.0 concatenate.4
  193.2 1.1 fusion.5
  194.4 0.3 copy.20
  194.7 4.5 %fusion.1 = f32[6,6]{0,1:T(8,128)S(1)} fusion(f32[1,64512]{1,0:T(1,128)S(1)} %bitcast.70, f32[5,64512]{1,0:T(8,128)S(1)} %bitcast.68), kind=kOutput, calls=%fused_computation.4 | convolution fusion | flops 28256256 | bytes 1548432 | tf_op jit(solution)/shard_map/dot_general | solution.py:54
  199.2 12.4 %psum.14 = f32[6,6]{0,1:T(8,128)S(1)} all-reduce(f32[6,6]{0,1:T(8,128)S(1)} %fusion.1), channel_id=1, replica_groups=mesh['row'=32,'col'=8] {'col'}, use_global_device_ids=true, to_apply=%region_5.6 | all-reduce | flops 36 | bytes 288 | tf_op jit(solution)/shard_map/psum | solution.py:55
  211.6 75.0 %psum.15 = f32[6,6]{0,1:T(8,128)S(1)} all-reduce(f32[6,6]{0,1:T(8,128)S(1)} %psum.14), channel_id=1, replica_groups=mesh['row'=32,'col'=8] {'row'}, use_global_device_ids=true, to_apply=%region_6.7 | all-reduce | flops 36 | bytes 288 | tf_op jit(solution)/shard_map/psum | solution.py:55
  286.5 0.1 copy.17
  286.6 0.5 cholesky.18
  287.2 0.6 compare_reduce_fusion
  287.8 0.6 select_select_fusion
  288.5 0.6 fusion.16
  289.1 0.7 fusion.15
  316.4 0.1 stack.27
  316.5 0.7 fusion.17
  317.2 0.0 copy-done.1
  317.2 0.0 copy-done.2
  317.2 4.6 %fusion.10 = f32[63,1024]{1,0:T(8,128)} fusion(bf16[5,63,1024]{2,1,0:T(8,128)(2,1)S(1)} %copy-done.2, f32[]{:T(128)} %bitcast.43, f32[]{:T(128)} %bitcast.41, f32[]{:T(128)} %bitcast.39, f32[]{:T(128)} %bitcast.37, f32[]{:T(128)} %bitcast.35, f32[]{:T(128)} %bitcast.34, f32[1024]{0:T(1024)S(1)} %add.49, f32[63]{0:T(128)S(1)} %add.48, ...), kind=kLoop, calls=%fused_computation.16 | loop fusion | flops 1225728 | bytes 1423640 | tf_op jit(solution)/shard_map/add | solution.py:59
  (7 shorter events, 0.1 us)
Async XLA Ops:
  6.5 56.4 %all-gather.3.cloned.1.call-start = ((), (), s32[]{:S(2)}) async-start(), calls=%async_computation | async-start | bytes 9437184 | tf_op jit(solution)/shard_map/all_gather | solution.py:42
  84.6 101.2 %copy-start.3 = (s32[2,63]{1,0:T(2,128)S(1)}, s32[2,63]{1,0:T(2,128)}, u32[]{:S(2)}) copy-start(s32[2,63]{1,0:T(2,128)} %param.16) | copy-start | bytes 1516
  183.7 2.1 copy-start
  183.8 3.0 copy-start.5
  183.8 4.1 %copy-start.4 = (f32[64]{0:T(128)S(1)}, f32[64]{0:T(128)}, u32[]{:S(2)}) copy-start(f32[64]{0:T(128)} %param.14) | copy-start | bytes 772
  183.8 7.4 %collective-permute-start = (f32[31,1024]{1,0:T(8,128)S(1)}, f32[31,1024]{1,0:T(8,128)}, u32[]{:S(2)}, u32[]{:S(2)}) collective-permute-start(f32[31,1024]{1,0:T(8,128)S(1)} %slice.172), channel_id=1, source_target_pairs={{0,8},{8,16},{16,24},{24,32},{32,40},{40,48},{48,56},{56,64},{64,7... | collective-permute-start | bytes 380936
  186.7 130.5 %copy-start.1 = (f32[63,1024]{1,0:T(8,128)S(1)}, f32[63,1024]{1,0:T(8,128)}, u32[]{:S(2)}) copy-start(f32[63,1024]{1,0:T(8,128)} %param.11) | copy-start | bytes 774148
  186.7 130.5 %copy-start.2 = (bf16[5,63,1024]{2,1,0:T(8,128)(2,1)S(1)}, bf16[5,63,1024]{2,1,0:T(8,128)(2,1)}, u32[]{:S(2)}) copy-start(bf16[5,63,1024]{2,1,0:T(8,128)(2,1)} %param.12) | copy-start | bytes 1935364
Sparse Core Ops, SparseCore 0:
  9.2 53.7 all-gather.2
